TPU v7x, 32 devices: a whole 2x2x4 slice. The times are simulated.
32 devices in a mesh: eq: 2 (over x), row: 4 (over y, core), col: 4 (over z).
Axes of the slice: x: 2, y: 2, z: 4, core: 2. Of those that a mesh axis runs over, the one named last changes fastest.
Arguments:
- transition: float32 [6144, 3072], P(('eq', 'row'), 'col'), parts along dimension 0, may hold values from -0.05 to 0.9
- covariance: float32 [6144, 3072], P(('eq', 'row'), 'col'), parts along dimension 0, may hold values from -1 to 5, as said below
Outputs:
- covariance_out: float32 [6144, 3072], P(('eq', 'row'), 'col'), parts along dimension 0
- transition_out: float32 [6144, 3072], P(('eq', 'row'), 'col'), parts along dimension 0
There are 2 independent parts, one for each index of `eq`. A program takes and returns all parts, laid end to end along the dimension named above; each array names one. Nothing has to cross between parts.
Inputs may be any that keep to these rules, and one draw needn't show every extreme that they name: covariance is exactly symmetric.
All inputs are finite; a program needn't handle non-finite values.
Results may differ from a plain program's by a relative error of at most 0.0001.
Values sent between devices are 32-bit elements; how exact they have to be, the bound alone decides.
No kernel may reach another device: no remote copies, remote signals or barrier semaphores. Data moves between devices by JAX's collectives and lax.ppermute only.
A program may use at most 128 MiB of HBM per device.

v0:
```python
import jax
import jax.numpy as jnp
from jax import lax
from jax.sharding import PartitionSpec as P


def per_device(transition, covariance):
    highest = lax.Precision.HIGHEST
    current = covariance
    matrix_row = lax.all_gather(transition, "col", axis=1, tiled=True)

    def add_one(pieces):
        return jnp.dot(matrix_row, pieces, precision=highest, preferred_element_type=jnp.float32)

    row_slices = lax.all_to_all(
        lax.all_to_all(transition, "row", split_axis=0, concat_axis=1, tiled=True),
        "col",
        split_axis=1,
        concat_axis=1,
        tiled=True,
    )
    product = add_one(lax.all_gather(current, "row", axis=0, tiled=True))
    squared = add_one(lax.all_gather(transition, "row", axis=0, tiled=True))
    product_row = lax.all_gather(product, "col", axis=1, tiled=True)
    update = lax.dot_general(
        product_row,
        lax.all_gather(row_slices, "row", axis=0, tiled=True),
        (((1,), (1,)), ((), ())),
        precision=highest,
        preferred_element_type=jnp.float32,
    )
    current = update + current
    return (current, squared)


def solution(mesh):
    return jax.shard_map(
        per_device,
        mesh=mesh,
        in_specs=(P(("eq", "row"), "col"), P(("eq", "row"), "col")),
        out_specs=(P(("eq", "row"), "col"), P(("eq", "row"), "col")),
        check_vma=False,
    )
```

profile of v0, /device:TPU:0, one launch (start us, length us, event | category | flops | bytes accessed | tf_op | source)
XLA Modules:
  0.0 605.5 jit_solution(9923091636029613894)
XLA Ops:
  7.2 0.0 all-gather.8.cloned.1.call-start
  7.2 0.7 all-gather.8.cloned.1.call-update
  7.9 0.0 all-gather.6.cloned.1.call-start
  7.9 0.7 all-gather.6.cloned.1.call-update
  8.6 0.0 all-gather.14.cloned.1.call-start
  8.7 0.7 all-gather.14.cloned.1.call-update
  9.4 0.0 all-gather.12.cloned.1.call-start
  9.4 51.7 %all_to_all.25 = f32[4,192,768]{2,1,0:T(8,128)S(1)} all-to-all(f32[4,192,768]{2,1,0:T(8,128)} %bitcast.10), channel_id=1, replica_groups=mesh['eq'=2,'row'=4,'col'=4] {'row'}, dimensions={0} | all-to-all | bytes 4718592 | tf_op jit(solution)/shard_map/all_to_all | solution.py:16
  61.1 88.7 %all_to_all.26 = f32[192,4,768]{2,0,1:T(8,128)S(1)} all-to-all(f32[192,4,768]{2,0,1:T(8,128)S(1)} %bitcast.13), channel_id=1, replica_groups=mesh['eq'=2,'row'=4,'col'=4] {'col'}, dimensions={1} | all-to-all | bytes 4718592 | tf_op jit(solution)/shard_map/all_to_all | solution.py:15
  149.8 1.6 copy.6
  151.5 0.0 all-gather.12.cloned.1.call-update
  151.5 0.0 all-gather.10.cloned.1.call-start
  151.5 0.0 all-gather.8.cloned.1.call-done
  151.6 121.3 %all-gather.6.cloned.1.call-done = f32[768,3072]{1,0:T(8,128)} async-done(((f32[768,768]{1,0:T(8,128)}), f32[768,3072]{1,0:T(8,128)}) %all-gather.6.cloned.1.call-update) | async-done | bytes 9437200 | tf_op jit(solution)/shard_map/all_gather | solution.py:10
  272.8 27.4 %fusion = f32[768,768]{1,0:T(8,128)} fusion(f32[768,3072]{1,0:T(8,128)} %all-gather.6.cloned.1.call-done, f32[3072,768]{1,0:T(8,128)} %all-gather.8.cloned.1.call-done), kind=kOutput, calls=%fused_computation.1 | convolution fusion | flops 21743271936 | bytes 21233664 | tf_op jit(solution)/shard_map/dot_general | solution.py:13
  300.2 0.0 all-gather.10.cloned.1.call-update
  300.3 0.0 copy-start
  300.3 36.6 %all-gather.14.cloned.1.call-done = f32[3072,768]{1,0:T(8,128)} async-done(((f32[768,768]{1,0:T(8,128)}), f32[3072,768]{1,0:T(8,128)}) %all-gather.14.cloned.1.call-update) | async-done | bytes 9437200 | tf_op jit(solution)/shard_map/all_gather | solution.py:23
  336.9 27.4 %fusion.1 = f32[768,768]{1,0:T(8,128)} fusion(f32[768,3072]{1,0:T(8,128)} %all-gather.6.cloned.1.call-done, f32[3072,768]{1,0:T(8,128)} %all-gather.14.cloned.1.call-done), kind=kOutput, calls=%fused_computation.2 | convolution fusion | flops 21743271936 | bytes 21233664 | tf_op jit(solution)/shard_map/dot_general | solution.py:13
  364.3 38.3 %all-gather.12.cloned.1.call-done = f32[768,3072]{1,0:T(8,128)} async-done(((f32[192,3072]{1,0:T(8,128)}), f32[768,3072]{1,0:T(8,128)}) %all-gather.12.cloned.1.call-update) | async-done | bytes 9437200 | tf_op jit(solution)/shard_map/all_gather | solution.py:27
  402.5 168.8 %all-gather.10.cloned.1.call-done = f32[768,3072]{1,0:T(8,128)} async-done(((f32[768,768]{1,0:T(8,128)}), f32[768,3072]{1,0:T(8,128)}) %all-gather.10.cloned.1.call-update) | async-done | bytes 9437200 | tf_op jit(solution)/shard_map/all_gather | solution.py:24
  571.3 0.0 copy-done
  571.3 27.7 %convolution_add_fusion = f32[768,768]{1,0:T(8,128)} fusion(f32[768,768]{1,0:T(8,128)S(1)} %copy-done, f32[768,3072]{1,0:T(8,128)} %all-gather.10.cloned.1.call-done, f32[768,3072]{1,0:T(8,128)} %all-gather.12.cloned.1.call-done), kind=kOutput, calls=%fused_computation | convolution fusion | flops 21743861760 | bytes 23592960 | tf_op jit(solution)/shard_map/dot_general | solution.py:25
Async XLA Ops:
  7.2 144.4 %all-gather.8.cloned.1.call-start = ((), (), s32[]{:S(2)}) async-start(), calls=%async_computation.3 | async-start | bytes 11796480 | tf_op jit(solution)/shard_map/all_gather | solution.py:22
  7.9 264.9 %all-gather.6.cloned.1.call-start = ((), (), s32[]{:S(2)}) async-start(), calls=%async_computation.2 | async-start | bytes 11796480 | tf_op jit(solution)/shard_map/all_gather | solution.py:10
  8.6 328.2 %all-gather.14.cloned.1.call-start = ((), (), s32[]{:S(2)}) async-start(), calls=%async_computation.6 | async-start | bytes 11796480 | tf_op jit(solution)/shard_map/all_gather | solution.py:23
  9.4 393.2 %all-gather.12.cloned.1.call-start = ((), (), s32[]{:S(2)}) async-start(), calls=%async_computation.5 | async-start | bytes 11796480 | tf_op jit(solution)/shard_map/all_gather | solution.py:27
  151.5 419.8 %all-gather.10.cloned.1.call-start = ((), (), s32[]{:S(2)}) async-start(), calls=%async_computation.4 | async-start | bytes 11796480 | tf_op jit(solution)/shard_map/all_gather | solution.py:24
  300.3 271.0 %copy-start = (f32[768,768]{1,0:T(8,128)S(1)}, f32[768,768]{1,0:T(8,128)}, u32[]{:S(2)}) copy-start(f32[768,768]{1,0:T(8,128)} %param.3) | copy-start | bytes 7077892
Sparse Core Ops, SparseCore 0:
  9.5 85.0 all-gather.7
  96.2 176.6 all-gather.5
  274.4 62.4 all-gather.13
  338.3 64.2 all-gather.11
  404.5 166.7 all-gather.9
where the time goes:
time: 606 us
  waiting for transfers between devices  367 us (61%)
  blocking collectives  140 us (23%)
  matrix products  82.5 us (14%)
  between operations  13.8 us (2%)
    all_gather x1, waiting for transfers between devices, per_device(): product_row = lax.all_gather(product, 'col', axis=1, tiled=True)  169 us
    all_gather x1, waiting for transfers between devices, per_device(): matrix_row = lax.all_gather(transition, 'col', axis=1, tiled=True)  121 us
    all_to_all x1, blocking collectives, per_device(): lax.all_to_all(lax.all_to_all(transition, 'row', split_axis=0, concat_axi...  88.7 us
    dot_general x2, matrix products, add_one(): jnp.dot(matrix_row, pieces, precision=highest, preferred_element_type=jnp...  54.8 us
    all_to_all x1, blocking collectives, per_device(): lax.all_to_all(transition, 'row', split_axis=0, concat_axis=1, tiled=True)  51.7 us
    all_gather x1, waiting for transfers between devices, per_device(): lax.all_gather(row_slices, 'row', axis=0, tiled=True)  38.3 us
    all_gather x1, waiting for transfers between devices, per_device(): squared = add_one(lax.all_gather(transition, 'row', axis=0, tiled=True))  36.6 us
    dot_general x1, matrix products, per_device(): lax.dot_general(product_row, lax.all_gather(row_slices, 'row', axis=0, ti...  27.7 us
  transfers between devices with their start and end apart: 5, of which 4 were waited for; matrix products, arithmetic and copies ran while one was open for 9% of the time, Pallas kernels for 0%

commit v1 on v0

--- a/solution.py
+++ b/solution.py
@@ -4,10 +4,21 @@
 from jax.sharding import PartitionSpec as P
 
 
+def pass_along(x, name, dim):
+    size = lax.axis_size(name)
+    hops = [(i, (i + 1) % size) for i in range(size)]
+    parts = [x]
+    for hop in range(1, size):
+        parts = [lax.ppermute(parts[0], name, hops), *parts]
+    result = jnp.concatenate(parts, axis=dim)
+    shift = (lax.axis_index(name) + 1) * parts[-1].shape[dim]
+    return jnp.roll(result, shift, axis=dim)
+
+
 def per_device(transition, covariance):
     highest = lax.Precision.HIGHEST
     current = covariance
-    matrix_row = lax.all_gather(transition, "col", axis=1, tiled=True)
+    matrix_row = pass_along(transition, "col", 1)
 
     def add_one(pieces):
         return jnp.dot(matrix_row, pieces, precision=highest, preferred_element_type=jnp.float32)

time: 606 us -> 527 us (0.87)
  waiting for transfers between devices: 367 us -> 296 us
  blocking collectives: 140 us -> 110 us
  local copies, waits for them, and re-layouts: 1.64 us -> 22.8 us
    ppermute x0 -> x3, waiting for transfers between devices: none -> 158 us  [pass_along(): parts = [lax.ppermute(parts[0], name, hops), *parts]]
    all_gather x1 -> x0, waiting for transfers between devices: 121 us -> none  [per_device(): matrix_row = lax.all_gather(transition, 'col', axis=1, tiled=True)]
    all_gather x1, waiting for transfers between devices: 38.3 us -> 0.01 us  [per_device(): lax.all_gather(row_slices, 'row', axis=0, tiled=True)]
    all_gather x1, waiting for transfers between devices: 36.6 us -> 0.02 us  [per_device(): squared = add_one(lax.all_gather(transition, 'row', axis=0, tiled=True))]
    all_gather x1, waiting for transfers between devices: 169 us -> 136 us  [per_device(): product_row = lax.all_gather(product, 'col', axis=1, tiled=True)]
    all_to_all x1, blocking collectives: 88.7 us -> 59.3 us  [per_device(): lax.all_to_all(lax.all_to_all(transition, 'row', split_axis=0, concat_axi...]
    unnamed x2 -> x15, local copies, waits for them, and re-layouts: 0.01 us -> 19.5 us
  transfers between devices with their start and end apart: 5 -> 7, of which waited for: 4 -> 4; matrix products, arithmetic and copies ran while one was open for 9% -> 15% of each run, Pallas kernels for 0% -> 0%
where the time goes in v1:
time: 527 us
  waiting for transfers between devices  296 us (56%)
  blocking collectives  110 us (21%)
  matrix products  83.2 us (16%)
  local copies, waits for them, and re-layouts  22.8 us (4%)
  between operations  13.8 us (3%)
    ppermute x3, waiting for transfers between devices, pass_along(): parts = [lax.ppermute(parts[0], name, hops), *parts]  158 us
    all_gather x1, waiting for transfers between devices, per_device(): product_row = lax.all_gather(product, 'col', axis=1, tiled=True)  136 us
    all_to_all x1, blocking collectives, per_device(): lax.all_to_all(lax.all_to_all(transition, 'row', split_axis=0, concat_axi...  59.3 us
    dot_general x2, matrix products, add_one(): jnp.dot(matrix_row, pieces, precision=highest, preferred_element_type=jnp...  55.5 us
    all_to_all x1, blocking collectives, per_device(): lax.all_to_all(transition, 'row', split_axis=0, concat_axis=1, tiled=True)  51 us
    dot_general x1, matrix products, per_device(): lax.dot_general(product_row, lax.all_gather(row_slices, 'row', axis=0, ti...  27.7 us
    unnamed x15, local copies, waits for them, and re-layouts  19.5 us
  transfers between devices with their start and end apart: 7, of which 4 were waited for; matrix products, arithmetic and copies ran while one was open for 15% of the time, Pallas kernels for 0%

profile of v1, /device:TPU:0, one launch (start us, length us, event | category | flops | bytes accessed | tf_op | source)
XLA Modules:
  0.0 526.7 jit_solution(3963260875512785808)
XLA Ops:
  7.2 0.0 all-gather.5.cloned.1.call-start
  7.2 0.7 all-gather.5.cloned.1.call-update
  7.9 0.0 all-gather.11.cloned.1.call-start
  8.0 0.7 all-gather.11.cloned.1.call-update
  8.7 0.0 all-gather.9.cloned.1.call-start
  8.7 51.0 %all_to_all.25 = f32[4,192,768]{2,1,0:T(8,128)S(1)} all-to-all(f32[4,192,768]{2,1,0:T(8,128)} %bitcast.8), channel_id=1, replica_groups=mesh['eq'=2,'row'=4,'col'=4] {'row'}, dimensions={0} | all-to-all | bytes 4718592 | tf_op jit(solution)/shard_map/all_to_all | solution.py:27
  59.7 59.3 %all_to_all.26 = f32[192,4,768]{2,0,1:T(8,128)S(1)} all-to-all(f32[192,4,768]{2,0,1:T(8,128)S(1)} %bitcast.11), channel_id=1, replica_groups=mesh['eq'=2,'row'=4,'col'=4] {'col'}, dimensions={1} | all-to-all | bytes 4718592 | tf_op jit(solution)/shard_map/all_to_all | solution.py:26
  119.0 1.6 copy.6
  120.7 0.0 all-gather.9.cloned.1.call-update
  120.7 0.0 all-gather.7.cloned.1.call-start
  120.8 0.3 collective-permute-start
  121.0 53.4 %collective-permute-done = f32[768,768]{1,0:T(8,128)S(1)} collective-permute-done((f32[768,768]{1,0:T(8,128)S(1)}, f32[768,768]{1,0:T(8,128)S(1)}, u32[]{:S(2)}, u32[]{:S(2)}) %collective-permute-start) | collective-permute-done | bytes 2359328 | tf_op jit(solution)/shard_map/ppermute | solution.py:12
  174.4 1.4 copy-done.1
  175.8 0.0 collective-permute-start.1
  175.8 52.8 %collective-permute-done.1 = f32[768,768]{1,0:T(8,128)} collective-permute-done((f32[768,768]{1,0:T(8,128)S(1)}, f32[768,768]{1,0:T(8,128)}, u32[]{:S(2)}, u32[]{:S(2)}) %collective-permute-start.1) | collective-permute-done | bytes 2359328 | tf_op jit(solution)/shard_map/ppermute | solution.py:12
  228.6 0.0 collective-permute-start.2
  228.6 52.2 %collective-permute-done.2 = f32[768,768]{1,0:T(8,128)} collective-permute-done((f32[768,768]{1,0:T(8,128)}, f32[768,768]{1,0:T(8,128)}, u32[]{:S(2)}, u32[]{:S(2)}) %collective-permute-start.2) | collective-permute-done | bytes 2359328 | tf_op jit(solution)/shard_map/ppermute | solution.py:12
  280.8 3.3 constant_dynamic-update-slice_fusion.7
  284.1 3.3 constant_dynamic-update-slice_fusion.6
  287.5 1.6 constant_dynamic-update-slice_fusion.5
  289.0 1.6 constant_dynamic-update-slice_fusion.4
  290.7 3.4 constant_dynamic-update-slice_fusion.3
  294.0 3.3 constant_dynamic-update-slice_fusion.2
  297.3 1.6 constant_dynamic-update-slice_fusion.1
  298.9 1.7 constant_dynamic-update-slice_fusion
  300.6 27.7 %fusion.2 = f32[768,768]{1,0:T(8,128)} fusion(f32[3072,768]{1,0:T(8,128)} %all-gather.5.cloned.1.call-done, f32[768,6144]{1,0:T(8,128)} %constant_dynamic-update-slice_fusion, s32[]{:T(128)S(6)} %select_n.14), kind=kOutput, calls=%fused_computation.2 | convolution fusion | flops 21743271936 | bytes 21233668 | tf_op jit(solution)/shard_map/dot_general | solution.py:24
  328.3 0.0 all-gather.7.cloned.1.call-update
  328.3 0.0 copy-start.3
  328.3 0.0 all-gather.11.cloned.1.call-done
  328.3 27.8 %fusion = f32[768,768]{1,0:T(8,128)} fusion(f32[3072,768]{1,0:T(8,128)} %all-gather.11.cloned.1.call-done, f32[768,6144]{1,0:T(8,128)} %constant_dynamic-update-slice_fusion, s32[]{:T(128)S(6)} %select_n.14), kind=kOutput, calls=%fused_computation | convolution fusion | flops 21743271936 | bytes 21233668 | tf_op jit(solution)/shard_map/dot_general | solution.py:24
  356.2 136.3 %all-gather.7.cloned.1.call-done = f32[768,3072]{1,0:T(8,128)} async-done(((f32[768,768]{1,0:T(8,128)}), f32[768,3072]{1,0:T(8,128)}) %all-gather.7.cloned.1.call-update) | async-done | bytes 9437200 | tf_op jit(solution)/shard_map/all_gather | solution.py:35
  492.5 27.7 %convolution_add_fusion = f32[768,768]{1,0:T(8,128)} fusion(f32[768,768]{1,0:T(8,128)S(1)} %copy-done.3, f32[768,3072]{1,0:T(8,128)} %all-gather.7.cloned.1.call-done, f32[768,3072]{1,0:T(8,128)} %all-gather.9.cloned.1.call-done), kind=kOutput, calls=%fused_computation.4 | convolution fusion | flops 21743861760 | bytes 23592960 | tf_op jit(solution)/shard_map/dot_general | solution.py:36
  (8 shorter events, 0.0 us)
Async XLA Ops:
  7.2 293.4 %all-gather.5.cloned.1.call-start = ((), (), s32[]{:S(2)}) async-start(), calls=%async_computation.2 | async-start | bytes 11796480 | tf_op jit(solution)/shard_map/all_gather | solution.py:33
  7.9 112.9 %copy-start = (f32[768,768]{1,0:T(8,128)S(1)}, f32[768,768]{1,0:T(8,128)}, u32[]{:S(2)}) copy-start(f32[768,768]{1,0:T(8,128)} %param.2) | copy-start | bytes 7077892
  7.9 320.4 %all-gather.11.cloned.1.call-start = ((), (), s32[]{:S(2)}) async-start(), calls=%async_computation.5 | async-start | bytes 11796480 | tf_op jit(solution)/shard_map/all_gather | solution.py:34
  8.7 347.5 %all-gather.9.cloned.1.call-start = ((), (), s32[]{:S(2)}) async-start(), calls=%async_computation.4 | async-start | bytes 11796480 | tf_op jit(solution)/shard_map/all_gather | solution.py:38
  120.7 371.8 %all-gather.7.cloned.1.call-start = ((), (), s32[]{:S(2)}) async-start(), calls=%async_computation.3 | async-start | bytes 11796480 | tf_op jit(solution)/shard_map/all_gather | solution.py:35
  120.8 53.6 %collective-permute-start = (f32[768,768]{1,0:T(8,128)S(1)}, f32[768,768]{1,0:T(8,128)S(1)}, u32[]{:S(2)}, u32[]{:S(2)}) collective-permute-start(f32[768,768]{1,0:T(8,128)S(1)} %copy-done), channel_id=1, source_target_pairs={{0,1},{1,2},{2,3},{3,0},{4,5},{5,6},{6,7},{7,4},{8,9},{9,10},{10,1... | collective-permute-start | bytes 7077896 | tf_op jit(solution)/shard_map/ppermute | solution.py:12
  174.4 1.4 copy-start.1
  175.8 52.8 %collective-permute-start.1 = (f32[768,768]{1,0:T(8,128)S(1)}, f32[768,768]{1,0:T(8,128)}, u32[]{:S(2)}, u32[]{:S(2)}) collective-permute-start(f32[768,768]{1,0:T(8,128)S(1)} %collective-permute-done), channel_id=1, source_target_pairs={{0,1},{1,2},{2,3},{3,0},{4,5},{5,6},{6,7},{7,4},{8,9},{9,10},{10,1... | collective-permute-start | bytes 7077896 | tf_op jit(solution)/shard_map/ppermute | solution.py:12
  228.6 52.2 %collective-permute-start.2 = (f32[768,768]{1,0:T(8,128)}, f32[768,768]{1,0:T(8,128)}, u32[]{:S(2)}, u32[]{:S(2)}) collective-permute-start(f32[768,768]{1,0:T(8,128)} %collective-permute-done.1), channel_id=1, source_target_pairs={{0,1},{1,2},{2,3},{3,0},{4,5},{5,6},{6,7},{7,4},{8,9},{9,10},{10,1... | collective-permute-start | bytes 7077896 | tf_op jit(solution)/shard_map/ppermute | solution.py:12
  228.6 58.8 %copy-start.2 = (f32[768,768]{1,0:T(8,128)S(1)}, f32[768,768]{1,0:T(8,128)}, u32[]{:S(2)}) copy-start(f32[768,768]{1,0:T(8,128)} %copy-done.1) | copy-start | bytes 7077892
  328.3 164.2 %copy-start.3 = (f32[768,768]{1,0:T(8,128)S(1)}, f32[768,768]{1,0:T(8,128)}, u32[]{:S(2)}) copy-start(f32[768,768]{1,0:T(8,128)} %param.3) | copy-start | bytes 7077892
Sparse Core Ops, SparseCore 0:
  9.5 84.3 all-gather.4
  95.4 65.2 all-gather.10
  162.3 64.2 all-gather.8
  328.4 164.0 all-gather.6
